TPU v7x, 32 devices: a whole 2x2x4 slice. The times are simulated.
32 devices in a mesh: lon: 8 (over y, x, core), lat: 4 (over z).
Axes of the slice: x: 2, y: 2, z: 4, core: 2. Of those that a mesh axis runs over, the one named last changes fastest.
Arguments:
- grid_latent: bfloat16 [4, 8, 1024, 512], P('lat', 'lon'), may hold values from -6 to 6
- mesh_latent: bfloat16 [4, 8, 160, 512], P('lat', 'lon'), may hold values from -6 to 6
- edge_geometry: float32 [4, 8, 4, 2048], P('lat', 'lon'), may hold values from -6 to 6
- senders: int32 [4, 8, 2048], P('lat', 'lon'), may hold values from 0 to 1023
- receivers: int32 [4, 8, 2048], P('lat', 'lon'), may hold values from 0 to 1439, as said below
- w_grid: bfloat16 [512, 512], replicated, may hold values from -0.25 to 0.25
- w_mesh: bfloat16 [512, 512], replicated, may hold values from -0.25 to 0.25
- w_edge: float32 [4, 512], replicated, may hold values from -3 to 3
- edge_bias: float32 [512], replicated, may hold values from -3 to 3
- w_message: bfloat16 [512, 512], replicated, may hold values from -0.25 to 0.25
- w_node: bfloat16 [1024, 512], replicated, may hold values from -0.1875 to 0.1875
- w_output: bfloat16 [512, 512], replicated, may hold values from -0.25 to 0.25
- norm_gain: float32 [512], replicated, may hold values from 0.1 to 1.9
- norm_bias: float32 [512], replicated, may hold values from -3 to 3
Outputs:
- mesh_out: bfloat16 [4, 8, 160, 512], P('lat', 'lon')
Inputs may be any that keep to these rules, and one draw needn't show every extreme that they name: `receivers`: r // 160 is a neighbour slot s from 0 to 8 (latitude offset s // 3 - 1, longitude offset s % 3 - 1); edges of the first band never name latitude offset -1, those of the last band never +1. For s other than 4, with k = s for s < 4 and k = s - 1 otherwise, the row r % 160 lies in k * 16 to k * 16 + 15 for s = 1, 3, 5, 7 and in k * 16 to k * 16 + 3 for s = 0, 2, 6, 8.
All inputs are finite; a program needn't handle non-finite values.
Results may differ from a plain program's by a relative error of at most 0.0095.
Values may be sent and summed in bfloat16 or wider, within the bound.
A program may use at most 64 MiB of HBM per device.

v0:
```python
import jax
import jax.numpy as jnp
from jax import lax
from jax.sharding import PartitionSpec as P

B_SIDE = 16


border_slots = (0, 1, 2, 3, 5, 6, 7, 8)


def extended(block, sides, width):
    for axis, dim in sides:
        count = lax.axis_size(axis)
        forward = [(i, i + 1) for i in range(count - 1)]
        forward.append((count - 1, 0))
        backward = [(target, source) for source, target in forward]
        low = lax.ppermute(
            lax.slice_in_dim(block, block.shape[dim] - width, None, axis=dim), axis, forward
        )
        high = lax.ppermute(lax.slice_in_dim(block, 0, width, axis=dim), axis, backward)
        block = jnp.concatenate([low, block, high], axis=dim)
    return block


def strip_of(block, slot):
    strip_number = slot if slot < 4 else slot - 1
    return block[strip_number * B_SIDE : (strip_number + 1) * B_SIDE]


def mirrored_cells(block):
    empty = jnp.zeros((B_SIDE, block.shape[1]), block.dtype)
    rows_out = []
    for lat_cell in range(3):
        cells = []
        for lon_cell in range(3):
            slot = (2 - lat_cell) * 3 + (2 - lon_cell)
            cells.append(empty if slot == 4 else strip_of(block, slot))
        rows_out.append(jnp.stack(cells))
    return jnp.stack(rows_out)


def local(
    grid_latent,
    mesh_latent,
    edge_geometry,
    senders,
    receivers,
    w_grid,
    w_mesh,
    w_edge,
    edge_bias,
    w_message,
    w_node,
    w_output,
    norm_gain,
    norm_bias,
):
    grid_rows = grid_latent[0, 0]
    own_mesh = mesh_latent[0, 0]
    geometry = edge_geometry[0, 0]
    sources = senders[0, 0]
    targets = receivers[0, 0]
    mesh_rows = own_mesh.shape[0]
    features = own_mesh.shape[1]
    edge_count = sources.shape[0]
    border_total = 8 * B_SIDE
    padded = extended(mirrored_cells(own_mesh), (("lon", 1), ("lat", 0)), 1)
    received = jnp.concatenate([padded[2 * (s // 3), 2 * (s % 3)] for s in border_slots], axis=0)
    mesh_table = jnp.dot(
        jnp.concatenate([own_mesh, received], axis=0), w_mesh, preferred_element_type=jnp.float32
    )
    slot_number = targets // mesh_rows
    row_number = targets % mesh_rows
    table_index = jnp.where(slot_number == 4, row_number, mesh_rows + row_number)
    slot_total = mesh_rows + border_total
    grid_proj = jnp.dot(grid_rows, w_grid, preferred_element_type=jnp.float32)
    edge_block = min(512, edge_count)
    block_count = edge_count // edge_block
    source_blocks = sources.reshape(block_count, edge_block)
    target_blocks = table_index.reshape(block_count, edge_block)
    geometry_blocks = jnp.transpose(geometry.reshape(4, block_count, edge_block), (1, 0, 2))
    slot_ids = jnp.arange(slot_total, dtype=jnp.int32)

    def add_block(summed, items):
        block_sources, block_targets, block_geometry = items
        grid_term = jnp.take(grid_proj, block_sources, axis=0)
        mesh_term = jnp.take(mesh_table, block_targets, axis=0)
        edge_term = jnp.dot(block_geometry.T, w_edge, precision=lax.Precision.HIGHEST)
        hidden = jax.nn.silu(grid_term + mesh_term + edge_term + edge_bias).astype(jnp.bfloat16)
        message = jnp.dot(hidden, w_message, preferred_element_type=jnp.float32).astype(
            jnp.bfloat16
        )
        target_onehot = (block_targets[:, None] == slot_ids[None, :]).astype(jnp.bfloat16)
        added = lax.dot_general(
            target_onehot, message, (((0,), (0,)), ((), ())), preferred_element_type=jnp.float32
        )
        return (summed + added, None)

    partial_value, _ = lax.scan(
        add_block,
        jnp.zeros((slot_total, features), jnp.float32),
        (source_blocks, target_blocks, geometry_blocks),
    )
    own_part = partial_value[:mesh_rows]
    border_part = partial_value[mesh_rows:]
    empty = jnp.zeros((B_SIDE, features), jnp.float32)
    cells = jnp.stack(
        [
            jnp.stack(
                [empty if a * 3 + b == 4 else strip_of(border_part, a * 3 + b) for b in range(3)]
            )
            for a in range(3)
        ]
    )
    padded = extended(cells.astype(jnp.bfloat16), (("lon", 1), ("lat", 0)), 1).astype(cells.dtype)
    arrived = jnp.concatenate(
        [padded[2 * (2 - s // 3), 2 * (2 - s % 3)] for s in border_slots], axis=0
    )
    arrived = jnp.concatenate(
        [arrived, jnp.zeros((mesh_rows - border_total, features), jnp.float32)], axis=0
    )
    aggregated = own_part + arrived
    node_in = jnp.concatenate([own_mesh, aggregated.astype(jnp.bfloat16)], axis=1)
    node_hidden = jax.nn.silu(jnp.dot(node_in, w_node, preferred_element_type=jnp.float32)).astype(
        jnp.bfloat16
    )
    update = jnp.dot(node_hidden, w_output, preferred_element_type=jnp.float32)
    row_mean = jnp.mean(update, axis=-1, keepdims=True)
    centered = update - row_mean
    row_var = jnp.mean(centered * centered, axis=-1, keepdims=True)
    normed = centered * lax.rsqrt(row_var + 1e-05) * norm_gain + norm_bias
    mesh_out = (own_mesh.astype(jnp.float32) + normed).astype(jnp.bfloat16)
    return mesh_out[None, None]


def solution(mesh):
    return jax.shard_map(
        local,
        mesh=mesh,
        in_specs=(
            P("lat", "lon", None, None),
            P("lat", "lon", None, None),
            P("lat", "lon", None, None),
            P("lat", "lon", None),
            P("lat", "lon", None),
            P(),
            P(),
            P(),
            P(),
            P(),
            P(),
            P(),
            P(),
            P(),
        ),
        out_specs=P("lat", "lon", None, None),
        check_vma=False,
    )
```

profile of v0, /device:TPU:0, one launch (start us, length us, event | category | flops | bytes accessed | tf_op | source)
XLA Modules:
  0.0 78.4 jit_solution(12093431954197767442)
XLA Ops:
  0.0 0.0 copy-start
  0.0 0.9 %slice_bitcast_fusion.31 = (bf16[1,16,512]{2,1,0:T(8,128)(2,1)S(1)}, bf16[1,16,512]{2,1,0:T(8,128)(2,1)S(1)}, bf16[1,16,512]{2,1,0:T(8,128)(2,1)S(1)}, bf16[1,16...) fusion(bf16[1,1,160,512]{3,2,1,0:T(8,128)(2,1)} %param.17), kind=kLoop, calls=%fused_computation.109 | loop fusion | bytes 262144 | tf_op jit(solution)/shard_map/stack | solution.py:39
  0.9 0.1 pad.38.clone
  1.0 0.1 maximum_bitcast_fusion
  1.1 0.5 collective-permute-start
  1.7 2.9 %collective-permute-start.1 = (bf16[3,1,16,512]{3,2,1,0:T(8,128)(2,1)S(1)}, bf16[3,1,16,512]{3,2,1,0:T(8,128)(2,1)S(1)}, u32[]{:S(2)}, u32[]{:S(2)}) collective-permute-start(bf16[3,1,16,512]{3,2,1,0:T(8,128)(2,1)S(1)} %get-tuple-element.149), channel_id=1, source_target_pairs={{4,0},{8,4},{12,8},{16,12},{20,16},{24,20},{28,24},{0,28},{5,1},{9... | collective-permute-start | bytes 147464 | tf_op jit(solution)/shard_map/ppermute | solution.py:21
  4.6 0.9 %constant_dynamic-update-slice_fusion.8 = bf16[288,512]{1,0:T(8,128)(2,1)S(1)} fusion(bf16[1,1,160,512]{3,2,1,0:T(8,128)(2,1)} %param.17), kind=kLoop, calls=%fused_computation.67 | loop fusion | bytes 327680
  5.5 0.0 copy-start.4
  5.5 0.8 divide_reduce_fusion
  6.3 0.0 copy-done
  6.3 0.0 copy-start.2
  6.3 0.0 copy-start.9
  6.3 0.0 copy-start.10
  6.4 3.1 %fusion.7 = f32[1024,512]{1,0:T(8,128)} fusion(bf16[512,512]{1,0:T(8,128)(2,1)} %param.21, bf16[1,1,1024,512]{3,2,1,0:T(8,128)(2,1)S(1)} %copy-done), kind=kOutput, calls=%fused_computation.23 | convolution fusion | flops 536870912 | bytes 3670016 | tf_op jit(solution)/shard_map/dot_general | solution.py:77
  9.5 0.0 copy-done.3
  9.6 0.0 collective-permute-done
  9.6 0.0 collective-permute-done.1
  9.6 2.3 %collective-permute-start.2 = (bf16[1,5,16,512]{3,2,1,0:T(8,128)(2,1)S(1)}, bf16[1,5,16,512]{3,2,1,0:T(8,128)(2,1)S(1)}, u32[]{:S(2)}, u32[]{:S(2)}) collective-permute-start(bf16[1,5,16,512]{3,2,1,0:T(8,128)(2,1)S(1)} %get-tuple-element.137), channel_id=1, source_target_pairs={{0,1},{1,2},{2,3},{3,0},{4,5},{5,6},{6,7},{7,4},{8,9},{9,10},{10,1... | collective-permute-start | bytes 245768 | tf_op jit(solution)/shard_map/ppermute | solution.py:18
  12.0 0.5 broadcast.127
  12.5 0.0 copy-done.4
  12.5 0.6 reduce.13
  13.1 2.1 %collective-permute-start.3 = (bf16[1,5,16,512]{3,2,1,0:T(8,128)(2,1)S(1)}, bf16[1,5,16,512]{3,2,1,0:T(8,128)(2,1)S(1)}, u32[]{:S(2)}, u32[]{:S(2)}) collective-permute-start(bf16[1,5,16,512]{3,2,1,0:T(8,128)(2,1)S(1)} %get-tuple-element.136), channel_id=1, source_target_pairs={{1,0},{2,1},{3,2},{0,3},{5,4},{6,5},{7,6},{4,7},{9,8},{10,9},{11,1... | collective-permute-start | bytes 245768 | tf_op jit(solution)/shard_map/ppermute | solution.py:21
  15.1 1.4 %collective-permute-done.2 = bf16[1,5,16,512]{3,2,1,0:T(8,128)(2,1)S(1)} collective-permute-done((bf16[1,5,16,512]{3,2,1,0:T(8,128)(2,1)S(1)}, bf16[1,5,16,512]{3,2,1,0:T(8,128)(2,1)S(1)}, u32[]{:S(2)}, u32[]{:S(2)}) %collective-permute-start.2) | collective-permute-done | bytes 81952 | tf_op jit(solution)/shard_map/ppermute | solution.py:18
  16.5 1.0 %collective-permute-done.3 = bf16[1,5,16,512]{3,2,1,0:T(8,128)(2,1)S(1)} collective-permute-done((bf16[1,5,16,512]{3,2,1,0:T(8,128)(2,1)S(1)}, bf16[1,5,16,512]{3,2,1,0:T(8,128)(2,1)S(1)}, u32[]{:S(2)}, u32[]{:S(2)}) %collective-permute-start.3) | collective-permute-done | bytes 81952 | tf_op jit(solution)/shard_map/ppermute | solution.py:21
  17.6 0.0 copy-done.2
  17.6 0.3 fusion.27
  17.9 0.0 copy-done.9
  17.9 0.0 copy-done.10
  17.9 45.8 %while.11 = (s32[]{:T(128)}, f32[288,512]{1,0:T(8,128)S(1)}, s32[4,512]{1,0:T(4,128)S(1)}, s32[4,512]{1,0:T(4,128)S(1)}, f32[1024,512]{1,0:T(8,128)}, /*index=5*...) while((s32[]{:T(128)}, f32[288,512]{1,0:T(8,128)S(1)}, ...), condition=%wide.region_1.2_spmd.clone, body=%wide.region_0.1_spmd.clone.sunk | while | flops 435350528 | bytes 9099907 | solution.py:100
  18.0 1.6 %gather_fusion = f32[512,512]{1,0:T(8,128)S(1)} fusion(f32[288,512]{1,0:T(8,128)S(1)} %get-tuple-element.252, s32[1024]{0:T(1024)S(1)} %pad_clamp_fusion.4), kind=kCustom, calls=%fused_computation.1.clone.clone.1 | custom fusion | bytes 2099200 | tf_op jit(solution)/shard_map/while/body/eval_jaxpr/jit(_take)/gather | solution.py:88
  19.6 4.3 %gather_fusion.1 = f32[512,512]{1,0:T(8,128)} fusion(f32[1024,512]{1,0:T(8,128)} %get-tuple-element.251, s32[1024]{0:T(1024)S(1)} %pad_clamp_fusion.5), kind=kCustom, calls=%fused_computation.clone.clone.1 | custom fusion | bytes 2099200 | tf_op jit(solution)/shard_map/while/body/eval_jaxpr/jit(_take)/gather | solution.py:87
  23.9 3.4 %multiply_convert_fusion.3 = bf16[512,512]{1,0:T(8,128)(2,1)} fusion(f32[4,512]{1,0:T(4,128)S(1)} %get-tuple-element.254, f32[512,512]{1,0:T(8,128)S(1)} %gather_fusion, f32[512,512]{1,0:T(8,128)} %gather_fusion.1, f32[512]{0:T(512)S(1)} %get-tuple-element.255, pred[512]{0:T(512)(128)(4,1)S(1)} %compare_and_fusion.4, ...), kind=kOutput, calls=%fused_computation.7.clone.1 | convolution fusion | flops 15204352 | bytes 2641408 | tf_op jit(solution)/shard_map/while/body/eval_jaxpr/dot_general | solution.py:89
  27.4 2.0 %convolution_add_fusion.3 = f32[288,512]{1,0:T(8,128)S(1)} fusion(bf16[512,512]{1,0:T(8,128)(2,1)} %multiply_convert_fusion.3, bf16[512,512]{1,0:T(8,128)(2,1)} %get-tuple-element.256, f32[288,512]{1,0:T(8,128)S(1)} %get-tuple-element.236, s32[512]{0:T(512)S(1)} %bitcast.159, pred[]{:T(512)S(6)} %compare.3), kind=kOutput, calls=%fused_computation.6.clone.1 | convolution fusion | flops 420134912 | bytes 2230273 | tf_op jit(solution)/shard_map/while/body/eval_jaxpr/dot_general | solution.py:95
  29.4 1.6 %gather_fusion = f32[512,512]{1,0:T(8,128)S(1)} fusion(f32[288,512]{1,0:T(8,128)S(1)} %get-tuple-element.252, s32[1024]{0:T(1024)S(1)} %pad_clamp_fusion.4), kind=kCustom, calls=%fused_computation.1.clone.clone.1 | custom fusion | bytes 2099200 | tf_op jit(solution)/shard_map/while/body/eval_jaxpr/jit(_take)/gather | solution.py:88
  31.1 4.3 %gather_fusion.1 = f32[512,512]{1,0:T(8,128)} fusion(f32[1024,512]{1,0:T(8,128)} %get-tuple-element.251, s32[1024]{0:T(1024)S(1)} %pad_clamp_fusion.5), kind=kCustom, calls=%fused_computation.clone.clone.1 | custom fusion | bytes 2099200 | tf_op jit(solution)/shard_map/while/body/eval_jaxpr/jit(_take)/gather | solution.py:87
  35.4 3.4 %multiply_convert_fusion.3 = bf16[512,512]{1,0:T(8,128)(2,1)} fusion(f32[4,512]{1,0:T(4,128)S(1)} %get-tuple-element.254, f32[512,512]{1,0:T(8,128)S(1)} %gather_fusion, f32[512,512]{1,0:T(8,128)} %gather_fusion.1, f32[512]{0:T(512)S(1)} %get-tuple-element.255, pred[512]{0:T(512)(128)(4,1)S(1)} %compare_and_fusion.4, ...), kind=kOutput, calls=%fused_computation.7.clone.1 | convolution fusion | flops 15204352 | bytes 2641408 | tf_op jit(solution)/shard_map/while/body/eval_jaxpr/dot_general | solution.py:89
  38.9 2.0 %convolution_add_fusion.3 = f32[288,512]{1,0:T(8,128)S(1)} fusion(bf16[512,512]{1,0:T(8,128)(2,1)} %multiply_convert_fusion.3, bf16[512,512]{1,0:T(8,128)(2,1)} %get-tuple-element.256, f32[288,512]{1,0:T(8,128)S(1)} %get-tuple-element.236, s32[512]{0:T(512)S(1)} %bitcast.159, pred[]{:T(512)S(6)} %compare.3), kind=kOutput, calls=%fused_computation.6.clone.1 | convolution fusion | flops 420134912 | bytes 2230273 | tf_op jit(solution)/shard_map/while/body/eval_jaxpr/dot_general | solution.py:95
  40.9 1.6 %gather_fusion = f32[512,512]{1,0:T(8,128)S(1)} fusion(f32[288,512]{1,0:T(8,128)S(1)} %get-tuple-element.252, s32[1024]{0:T(1024)S(1)} %pad_clamp_fusion.4), kind=kCustom, calls=%fused_computation.1.clone.clone.1 | custom fusion | bytes 2099200 | tf_op jit(solution)/shard_map/while/body/eval_jaxpr/jit(_take)/gather | solution.py:88
  42.5 4.3 %gather_fusion.1 = f32[512,512]{1,0:T(8,128)} fusion(f32[1024,512]{1,0:T(8,128)} %get-tuple-element.251, s32[1024]{0:T(1024)S(1)} %pad_clamp_fusion.5), kind=kCustom, calls=%fused_computation.clone.clone.1 | custom fusion | bytes 2099200 | tf_op jit(solution)/shard_map/while/body/eval_jaxpr/jit(_take)/gather | solution.py:87
  46.9 3.4 %multiply_convert_fusion.3 = bf16[512,512]{1,0:T(8,128)(2,1)} fusion(f32[4,512]{1,0:T(4,128)S(1)} %get-tuple-element.254, f32[512,512]{1,0:T(8,128)S(1)} %gather_fusion, f32[512,512]{1,0:T(8,128)} %gather_fusion.1, f32[512]{0:T(512)S(1)} %get-tuple-element.255, pred[512]{0:T(512)(128)(4,1)S(1)} %compare_and_fusion.4, ...), kind=kOutput, calls=%fused_computation.7.clone.1 | convolution fusion | flops 15204352 | bytes 2641408 | tf_op jit(solution)/shard_map/while/body/eval_jaxpr/dot_general | solution.py:89
  50.3 2.0 %convolution_add_fusion.3 = f32[288,512]{1,0:T(8,128)S(1)} fusion(bf16[512,512]{1,0:T(8,128)(2,1)} %multiply_convert_fusion.3, bf16[512,512]{1,0:T(8,128)(2,1)} %get-tuple-element.256, f32[288,512]{1,0:T(8,128)S(1)} %get-tuple-element.236, s32[512]{0:T(512)S(1)} %bitcast.159, pred[]{:T(512)S(6)} %compare.3), kind=kOutput, calls=%fused_computation.6.clone.1 | convolution fusion | flops 420134912 | bytes 2230273 | tf_op jit(solution)/shard_map/while/body/eval_jaxpr/dot_general | solution.py:95
  52.3 1.6 %gather_fusion = f32[512,512]{1,0:T(8,128)S(1)} fusion(f32[288,512]{1,0:T(8,128)S(1)} %get-tuple-element.252, s32[1024]{0:T(1024)S(1)} %pad_clamp_fusion.4), kind=kCustom, calls=%fused_computation.1.clone.clone.1 | custom fusion | bytes 2099200 | tf_op jit(solution)/shard_map/while/body/eval_jaxpr/jit(_take)/gather | solution.py:88
  54.0 4.3 %gather_fusion.1 = f32[512,512]{1,0:T(8,128)} fusion(f32[1024,512]{1,0:T(8,128)} %get-tuple-element.251, s32[1024]{0:T(1024)S(1)} %pad_clamp_fusion.5), kind=kCustom, calls=%fused_computation.clone.clone.1 | custom fusion | bytes 2099200 | tf_op jit(solution)/shard_map/while/body/eval_jaxpr/jit(_take)/gather | solution.py:87
  58.3 3.4 %multiply_convert_fusion.3 = bf16[512,512]{1,0:T(8,128)(2,1)} fusion(f32[4,512]{1,0:T(4,128)S(1)} %get-tuple-element.254, f32[512,512]{1,0:T(8,128)S(1)} %gather_fusion, f32[512,512]{1,0:T(8,128)} %gather_fusion.1, f32[512]{0:T(512)S(1)} %get-tuple-element.255, pred[512]{0:T(512)(128)(4,1)S(1)} %compare_and_fusion.4, ...), kind=kOutput, calls=%fused_computation.7.clone.1 | convolution fusion | flops 15204352 | bytes 2641408 | tf_op jit(solution)/shard_map/while/body/eval_jaxpr/dot_general | solution.py:89
  61.8 2.0 %convolution_add_fusion.3 = f32[288,512]{1,0:T(8,128)S(1)} fusion(bf16[512,512]{1,0:T(8,128)(2,1)} %multiply_convert_fusion.3, bf16[512,512]{1,0:T(8,128)(2,1)} %get-tuple-element.256, f32[288,512]{1,0:T(8,128)S(1)} %get-tuple-element.236, s32[512]{0:T(512)S(1)} %bitcast.159, pred[]{:T(512)S(6)} %compare.3), kind=kOutput, calls=%fused_computation.6.clone.1 | convolution fusion | flops 420134912 | bytes 2230273 | tf_op jit(solution)/shard_map/while/body/eval_jaxpr/dot_general | solution.py:95
  63.8 0.0 copy-start.1
  63.8 0.0 copy-start.7
  63.8 0.0 copy-start.8
  63.9 0.1 maximum_bitcast_fusion.4
  64.0 0.1 collective-permute-start.4
  64.1 2.6 %collective-permute-start.5 = (bf16[3,1,16,512]{3,2,1,0:T(8,128)(2,1)S(1)}, bf16[3,1,16,512]{3,2,1,0:T(8,128)(2,1)S(1)}, u32[]{:S(2)}, u32[]{:S(2)}) collective-permute-start(bf16[3,1,16,512]{3,2,1,0:T(8,128)(2,1)S(1)} %get-tuple-element.147), channel_id=1, source_target_pairs={{4,0},{8,4},{12,8},{16,12},{20,16},{24,20},{28,24},{0,28},{5,1},{9... | collective-permute-start | bytes 147464 | tf_op jit(solution)/shard_map/ppermute | solution.py:21
  66.7 1.8 %collective-permute-done.4 = bf16[3,1,16,512]{3,2,1,0:T(8,128)(2,1)S(1)} collective-permute-done((bf16[3,1,16,512]{3,2,1,0:T(8,128)(2,1)S(1)}, bf16[3,1,16,512]{3,2,1,0:T(8,128)(2,1)S(1)}, u32[]{:S(2)}, u32[]{:S(2)}) %collective-permute-start.4) | collective-permute-done | bytes 49184 | tf_op jit(solution)/shard_map/ppermute | solution.py:18
  68.5 0.0 collective-permute-done.5
  68.5 1.6 %collective-permute-start.6 = (bf16[1,5,16,512]{3,2,1,0:T(8,128)(2,1)S(1)}, bf16[1,5,16,512]{3,2,1,0:T(8,128)(2,1)S(1)}, u32[]{:S(2)}, u32[]{:S(2)}) collective-permute-start(bf16[1,5,16,512]{3,2,1,0:T(8,128)(2,1)S(1)} %get-tuple-element.134), channel_id=1, source_target_pairs={{0,1},{1,2},{2,3},{3,0},{4,5},{5,6},{6,7},{7,4},{8,9},{9,10},{10,1... | collective-permute-start | bytes 245768 | tf_op jit(solution)/shard_map/ppermute | solution.py:18
  70.1 2.3 %collective-permute-start.7 = (bf16[1,5,16,512]{3,2,1,0:T(8,128)(2,1)S(1)}, bf16[1,5,16,512]{3,2,1,0:T(8,128)(2,1)S(1)}, u32[]{:S(2)}, u32[]{:S(2)}) collective-permute-start(bf16[1,5,16,512]{3,2,1,0:T(8,128)(2,1)S(1)} %get-tuple-element.135), channel_id=1, source_target_pairs={{1,0},{2,1},{3,2},{0,3},{5,4},{6,5},{7,6},{4,7},{9,8},{10,9},{11,1... | collective-permute-start | bytes 245768 | tf_op jit(solution)/shard_map/ppermute | solution.py:21
  72.4 3.2 %collective-permute-done.6 = bf16[1,5,16,512]{3,2,1,0:T(8,128)(2,1)S(1)} collective-permute-done((bf16[1,5,16,512]{3,2,1,0:T(8,128)(2,1)S(1)}, bf16[1,5,16,512]{3,2,1,0:T(8,128)(2,1)S(1)}, u32[]{:S(2)}, u32[]{:S(2)}) %collective-permute-start.6) | collective-permute-done | bytes 81952 | tf_op jit(solution)/shard_map/ppermute | solution.py:18
  75.7 0.6 collective-permute-done.7
  76.3 0.1 maximum_convert_fusion
  76.5 0.1 add_convert_fusion.1
  76.6 0.0 copy-start.5
  76.6 0.0 copy-start.6
  76.6 0.7 fusion.24
  77.3 0.2 multiply_reduce_fusion
  77.6 0.8 %fusion.18 = bf16[1,1,160,512]{3,2,1,0:T(8,128)(2,1)} fusion(f32[160,512]{1,0:T(8,128)S(1)} %get-tuple-element.151, f32[512]{0:T(512)S(1)} %copy-done.5, f32[512]{0:T(512)S(1)} %copy-done.6, f32[160]{0:T(256)S(1)} %add_rsqrt_fusion, f32[160]{0:T(256)S(1)} %broadcast_multiply_fusion, bf16[1,1,160,512]{3,2,1,0:T(8,128)(2,1)S(1)} %copy-done.1), kind=kLoop, calls=%fused_computation.35 | loop fusion | flops 573440 | bytes 660736 | tf_op jit(solution)/shard_map/broadcast_in_dim | solution.py:134
  (61 shorter events, 0.5 us)
Async XLA Ops:
  0.0 6.3 %copy-start = (bf16[1,1,1024,512]{3,2,1,0:T(8,128)(2,1)S(1)}, bf16[1,1,1024,512]{3,2,1,0:T(8,128)(2,1)}, u32[]{:S(2)}) copy-start(bf16[1,1,1024,512]{3,2,1,0:T(8,128)(2,1)} %param.16) | copy-start | bytes 3145732
  1.1 8.4 %copy-start.3 = (s32[1,1,2048]{2,1,0:T(1,128)S(1)}, s32[1,1,2048]{2,1,0:T(1,128)}, u32[]{:S(2)}) copy-start(s32[1,1,2048]{2,1,0:T(1,128)} %param.20) | copy-start | bytes 24580
  1.1 8.5 %collective-permute-start = (bf16[3,1,16,512]{3,2,1,0:T(8,128)(2,1)S(1)}, bf16[3,1,16,512]{3,2,1,0:T(8,128)(2,1)S(1)}, u32[]{:S(2)}, u32[]{:S(2)}) collective-permute-start(bf16[3,1,16,512]{3,2,1,0:T(8,128)(2,1)S(1)} %get-tuple-element.148), channel_id=1, source_target_pairs={{0,4},{4,8},{8,12},{12,16},{16,20},{20,24},{24,28},{28,0},{1,5},{5... | collective-permute-start | bytes 147464 | tf_op jit(solution)/shard_map/ppermute | solution.py:18
  1.7 7.9 %collective-permute-start.1 = (bf16[3,1,16,512]{3,2,1,0:T(8,128)(2,1)S(1)}, bf16[3,1,16,512]{3,2,1,0:T(8,128)(2,1)S(1)}, u32[]{:S(2)}, u32[]{:S(2)}) collective-permute-start(bf16[3,1,16,512]{3,2,1,0:T(8,128)(2,1)S(1)} %get-tuple-element.149), channel_id=1, source_target_pairs={{4,0},{8,4},{12,8},{16,12},{20,16},{24,20},{28,24},{0,28},{5,1},{9... | collective-permute-start | bytes 147464 | tf_op jit(solution)/shard_map/ppermute | solution.py:21
  5.5 6.9 %copy-start.4 = (s32[1,1,2048]{2,1,0:T(1,128)S(1)}, s32[1,1,2048]{2,1,0:T(1,128)}, u32[]{:S(2)}) copy-start(s32[1,1,2048]{2,1,0:T(1,128)} %param.19) | copy-start | bytes 24580
  6.3 11.2 %copy-start.2 = (bf16[512,512]{1,0:T(8,128)(2,1)S(1)}, bf16[512,512]{1,0:T(8,128)(2,1)}, u32[]{:S(2)}) copy-start(bf16[512,512]{1,0:T(8,128)(2,1)} %param.22) | copy-start | bytes 1572868
  6.3 11.6 %copy-start.9 = (f32[4,512]{1,0:T(4,128)S(1)}, f32[4,512]{1,0:T(4,128)}, u32[]{:S(2)}) copy-start(f32[4,512]{1,0:T(4,128)} %param.23) | copy-start | bytes 24580
  6.3 11.6 %copy-start.10 = (f32[512]{0:T(512)S(1)}, f32[512]{0:T(512)}, u32[]{:S(2)}) copy-start(f32[512]{0:T(512)} %param.24) | copy-start | bytes 6148
  9.6 6.9 %collective-permute-start.2 = (bf16[1,5,16,512]{3,2,1,0:T(8,128)(2,1)S(1)}, bf16[1,5,16,512]{3,2,1,0:T(8,128)(2,1)S(1)}, u32[]{:S(2)}, u32[]{:S(2)}) collective-permute-start(bf16[1,5,16,512]{3,2,1,0:T(8,128)(2,1)S(1)} %get-tuple-element.137), channel_id=1, source_target_pairs={{0,1},{1,2},{2,3},{3,0},{4,5},{5,6},{6,7},{7,4},{8,9},{9,10},{10,1... | collective-permute-start | bytes 245768 | tf_op jit(solution)/shard_map/ppermute | solution.py:18
  13.1 4.5 %collective-permute-start.3 = (bf16[1,5,16,512]{3,2,1,0:T(8,128)(2,1)S(1)}, bf16[1,5,16,512]{3,2,1,0:T(8,128)(2,1)S(1)}, u32[]{:S(2)}, u32[]{:S(2)}) collective-permute-start(bf16[1,5,16,512]{3,2,1,0:T(8,128)(2,1)S(1)} %get-tuple-element.136), channel_id=1, source_target_pairs={{1,0},{2,1},{3,2},{0,3},{5,4},{6,5},{7,6},{4,7},{9,8},{10,9},{11,1... | collective-permute-start | bytes 245768 | tf_op jit(solution)/shard_map/ppermute | solution.py:21
  63.8 12.8 %copy-start.1 = (bf16[1,1,160,512]{3,2,1,0:T(8,128)(2,1)S(1)}, bf16[1,1,160,512]{3,2,1,0:T(8,128)(2,1)}, u32[]{:S(2)}) copy-start(bf16[1,1,160,512]{3,2,1,0:T(8,128)(2,1)} %param.17) | copy-start | bytes 491524
  63.8 12.8 %copy-start.7 = (bf16[1024,512]{1,0:T(8,128)(2,1)S(1)}, bf16[1024,512]{1,0:T(8,128)(2,1)}, u32[]{:S(2)}) copy-start(bf16[1024,512]{1,0:T(8,128)(2,1)} %param.26) | copy-start | bytes 3145732
  63.8 12.8 %copy-start.8 = (bf16[512,512]{1,0:T(8,128)(2,1)S(1)}, bf16[512,512]{1,0:T(8,128)(2,1)}, u32[]{:S(2)}) copy-start(bf16[512,512]{1,0:T(8,128)(2,1)} %param.27) | copy-start | bytes 1572868
  64.0 4.5 %collective-permute-start.4 = (bf16[3,1,16,512]{3,2,1,0:T(8,128)(2,1)S(1)}, bf16[3,1,16,512]{3,2,1,0:T(8,128)(2,1)S(1)}, u32[]{:S(2)}, u32[]{:S(2)}) collective-permute-start(bf16[3,1,16,512]{3,2,1,0:T(8,128)(2,1)S(1)} %get-tuple-element.146), channel_id=1, source_target_pairs={{0,4},{4,8},{8,12},{12,16},{16,20},{20,24},{24,28},{28,0},{1,5},{5... | collective-permute-start | bytes 147464 | tf_op jit(solution)/shard_map/ppermute | solution.py:18
  64.1 4.4 %collective-permute-start.5 = (bf16[3,1,16,512]{3,2,1,0:T(8,128)(2,1)S(1)}, bf16[3,1,16,512]{3,2,1,0:T(8,128)(2,1)S(1)}, u32[]{:S(2)}, u32[]{:S(2)}) collective-permute-start(bf16[3,1,16,512]{3,2,1,0:T(8,128)(2,1)S(1)} %get-tuple-element.147), channel_id=1, source_target_pairs={{4,0},{8,4},{12,8},{16,12},{20,16},{24,20},{28,24},{0,28},{5,1},{9... | collective-permute-start | bytes 147464 | tf_op jit(solution)/shard_map/ppermute | solution.py:21
  68.5 7.2 %collective-permute-start.6 = (bf16[1,5,16,512]{3,2,1,0:T(8,128)(2,1)S(1)}, bf16[1,5,16,512]{3,2,1,0:T(8,128)(2,1)S(1)}, u32[]{:S(2)}, u32[]{:S(2)}) collective-permute-start(bf16[1,5,16,512]{3,2,1,0:T(8,128)(2,1)S(1)} %get-tuple-element.134), channel_id=1, source_target_pairs={{0,1},{1,2},{2,3},{3,0},{4,5},{5,6},{6,7},{7,4},{8,9},{9,10},{10,1... | collective-permute-start | bytes 245768 | tf_op jit(solution)/shard_map/ppermute | solution.py:18
  70.1 6.2 %collective-permute-start.7 = (bf16[1,5,16,512]{3,2,1,0:T(8,128)(2,1)S(1)}, bf16[1,5,16,512]{3,2,1,0:T(8,128)(2,1)S(1)}, u32[]{:S(2)}, u32[]{:S(2)}) collective-permute-start(bf16[1,5,16,512]{3,2,1,0:T(8,128)(2,1)S(1)} %get-tuple-element.135), channel_id=1, source_target_pairs={{1,0},{2,1},{3,2},{0,3},{5,4},{6,5},{7,6},{4,7},{9,8},{10,9},{11,1... | collective-permute-start | bytes 245768 | tf_op jit(solution)/shard_map/ppermute | solution.py:21
  76.6 1.0 %copy-start.5 = (f32[512]{0:T(512)S(1)}, f32[512]{0:T(512)}, u32[]{:S(2)}) copy-start(f32[512]{0:T(512)} %param.29) | copy-start | bytes 6148
  76.6 1.0 %copy-start.6 = (f32[512]{0:T(512)S(1)}, f32[512]{0:T(512)}, u32[]{:S(2)}) copy-start(f32[512]{0:T(512)} %param.28) | copy-start | bytes 6148
where the time goes:
time: 78.9 us; the launch traced here: 78.4 us
  local copies, waits for them, and re-layouts  26.4 us (33%)
  matrix products  25.8 us (33%)
  starting transfers between devices  14.5 us (18%)
  waiting for transfers between devices  8.01 us (10%)
  other arithmetic  3.05 us (4%)
    gather x4, local copies, waits for them, and re-layouts, add_block(): grid_term = jnp.take(grid_proj, block_sources, axis=0)  17.3 us
    dot_general x4, matrix products, add_block(): jnp.dot(block_geometry.T, w_edge, precision=lax.Precision.HIGHEST)  13.8 us
    ppermute x4, starting transfers between devices, extended(): lax.ppermute(lax.slice_in_dim(block, 0, width, axis=dim), axis, backward)  9.99 us
    dot_general x4, matrix products, add_block(): lax.dot_general(target_onehot, message, (((0,), (0,)), ((), ())), preferr...  7.88 us
    gather x4, local copies, waits for them, and re-layouts, add_block(): mesh_term = jnp.take(mesh_table, block_targets, axis=0)  6.48 us
    ppermute x4, waiting for transfers between devices, extended(): lax.ppermute(lax.slice_in_dim(block, block.shape[dim] - width, None, axis...  6.36 us
    ppermute x4, starting transfers between devices, extended(): lax.ppermute(lax.slice_in_dim(block, block.shape[dim] - width, None, axis...  4.56 us
    dot_general x1, matrix products, local(): grid_proj = jnp.dot(grid_rows, w_grid, preferred_element_type=jnp.float32)  3.13 us
  transfers between devices with their start and end apart: 8, of which 5 were waited for; matrix products, arithmetic and copies ran while one was open for 8% of the time, Pallas kernels for 0%

commit v1 on v0

v1 whole, which is shorter than its diff:
```python
import functools

import jax
import jax.numpy as jnp
from jax import lax
from jax.experimental import pallas as pl
from jax.experimental.pallas import tpu as pltpu
from jax.sharding import PartitionSpec as P

B_SIDE = 16
B_CORNER = 4
TAIL = 16
MESH = pl.DeviceIdType.MESH

BF16 = jnp.bfloat16
F32 = jnp.float32

STRIPS = tuple((s, s if s < 4 else s - 1) for s in range(9) if s != 4)
SIDES = (1, 3, 5, 7)
CORNERS = (0, 2, 6, 8)


def nt(a, b):
    return lax.dot_general(a, b, (((1,), (1,)), ((), ())), preferred_element_type=F32)


def nn(a, b):
    return jnp.dot(a, b, preferred_element_type=F32)


def halves(x):
    high = x.astype(BF16)
    return high, (x - high.astype(F32)).astype(BF16)


def kernel(
    n_lon,
    n_lat,
    grid_h,
    mesh_h,
    geo_h,
    snd_h,
    rcv_h,
    w_grid_h,
    w_mesh_h,
    w_edge_h,
    bias_h,
    w_message_h,
    w_node_h,
    w_output_h,
    gain_h,
    nbias_h,
    out_ref,
    grid_v,
    mesh_v,
    geo_v,
    snd_v,
    rcv_v,
    w_grid_v,
    w_mesh_v,
    w_edge_v,
    bias_v,
    w_message_v,
    w_node_v,
    w_output_v,
    gain_v,
    nbias_v,
    table,
    onehot,
    summed,
    got_mesh,
    put_sum,
    got_sum,
    load_sem,
    send_a,
    recv_a,
    send_b,
    recv_b,
):
    lon = lax.axis_index("lon")
    lat = lax.axis_index("lat")
    rows, features = mesh_v.shape
    grid_rows = grid_v.shape[0]
    edges = snd_v.shape[1]
    side_base = rows
    corner_base = rows + 4 * B_SIDE
    slots = corner_base + 4 * B_CORNER

    sources = [
        (mesh_h.at[0, 0], mesh_v),
        (snd_h.at[0], snd_v),
        (rcv_h.at[0], rcv_v),
        (geo_h.at[0, 0], geo_v),
        (w_edge_h, w_edge_v),
        (bias_h, bias_v),
        (w_grid_h, w_grid_v),
        (grid_h.at[0, 0], grid_v),
        (w_mesh_h, w_mesh_v),
        (w_node_h, w_node_v),
        (w_message_h, w_message_v),
        (w_output_h, w_output_v),
        (gain_h, gain_v),
        (nbias_h, nbias_v),
    ]
    loads = {}
    for number, (source, target) in enumerate(sources):
        copy = pltpu.make_async_copy(source, target, load_sem.at[number])
        copy.start()
        loads[id(target)] = copy

    def loaded(ref):
        loads[id(ref)].wait()

    def there(dlat, dlon):
        return {
            "lat": lat + dlat,
            "lon": lax.rem(lon + dlon + n_lon, n_lon),
        }

    def has(dlat):
        if dlat == 0:
            return None
        return lat > 0 if dlat < 0 else lat < n_lat - 1

    def guarded(dlat, body, other=None):
        condition = has(dlat)
        if condition is None:
            body()
            return
        pl.when(condition)(body)
        if other is not None:
            pl.when(jnp.logical_not(condition))(other)

    barrier = pltpu.get_barrier_semaphore()
    for dlat in (0, -1, 1):

        def greet(dlat=dlat):
            for dlon in (-1, 0, 1):
                if (dlat, dlon) != (0, 0):
                    pl.semaphore_signal(
                        barrier, inc=1, device_id=there(dlat, dlon), device_id_type=MESH
                    )

        guarded(dlat, greet)
    arrivals = 2 + 3 * (lat > 0).astype(jnp.int32) + 3 * (lat < n_lat - 1).astype(jnp.int32)
    pl.semaphore_wait(barrier, arrivals)

    def mesh_copy(slot, k):
        return pltpu.make_async_remote_copy(
            src_ref=mesh_v.at[pl.ds(k * B_SIDE, B_SIDE)],
            dst_ref=got_mesh.at[k],
            send_sem=send_a.at[k],
            recv_sem=recv_a.at[k],
            device_id=there(-(slot // 3 - 1), -(slot % 3 - 1)),
            device_id_type=MESH,
        )

    def sum_copy(slot, k):
        return pltpu.make_async_remote_copy(
            src_ref=put_sum.at[k],
            dst_ref=got_sum.at[k],
            send_sem=send_b.at[k],
            recv_sem=recv_b.at[k],
            device_id=there(slot // 3 - 1, slot % 3 - 1),
            device_id_type=MESH,
        )

    def in_band(dlat):
        return [(s, k) for s, k in STRIPS if s // 3 - 1 == dlat]

    loaded(mesh_v)
    for dlat in (-1, 1, 0):

        def send(dlat=dlat):
            for s, k in in_band(dlat):
                mesh_copy(s, k).start()

        guarded(-dlat, send)

    loaded(snd_v)
    loaded(rcv_v)
    loaded(geo_v)
    picks = rcv_v[...]
    shift, spot = 0, picks
    for s in range(9):
        k = s if s < 4 else s - 1
        if s == 4:
            base = -4 * rows
        elif s in SIDES:
            base = side_base + B_SIDE * SIDES.index(s) - k * B_SIDE - s * rows
        else:
            base = corner_base + B_CORNER * CORNERS.index(s) - k * B_SIDE - s * rows
        if s == 0:
            spot = spot + base
        else:
            spot = spot + jnp.where(picks >= s * rows, base - shift, 0)
        shift = base
    step = min(512, edges)
    for start in range(0, edges, step):
        span = pl.ds(start, step)
        ids = lax.broadcasted_iota(jnp.int32, (grid_rows, step), 0)
        onehot[:grid_rows, span] = jnp.where(ids == snd_v[:, span], 1.0, 0.0).astype(BF16)
        ids = lax.broadcasted_iota(jnp.int32, (slots, step), 0)
        onehot[grid_rows : grid_rows + slots, span] = jnp.where(
            ids == spot[:, start : start + step], 1.0, 0.0
        ).astype(BF16)
    high, low = [part.astype(F32) for part in halves(geo_v[...])]
    ones = jnp.ones((2, edges), F32)
    zeros = jnp.zeros((2, edges), F32)
    onehot[grid_rows + slots :, :] = jnp.concatenate([high, high, low, ones, zeros], 0).astype(BF16)

    loaded(w_grid_v)
    loaded(grid_v)
    w_grid_t = jnp.transpose(w_grid_v[...])
    table[:, :grid_rows] = (0.5 * nt(w_grid_t, grid_v[...])).astype(BF16)

    loaded(w_edge_v)
    loaded(bias_v)
    high, low = [part.astype(F32) for part in halves(w_edge_v[...])]
    bias_high, bias_low = [part.astype(F32) for part in halves(bias_v[...])]
    tail = jnp.concatenate(
        [high, low, high, bias_high, bias_low, jnp.zeros((2, features), F32)], 0
    )
    loaded(w_mesh_v)
    loaded(w_node_v)
    node_own = nn(mesh_v[...], w_node_v[:features, :])

    for dlat in (-1, 0, 1):

        def arrive(dlat=dlat):
            for s, k in in_band(dlat):
                mesh_copy(s, k).wait_recv()

        def nothing(dlat=dlat):
            for s, k in in_band(dlat):
                got_mesh[k] = jnp.zeros(got_mesh.shape[1:], BF16)

        guarded(dlat, arrive, nothing)

    strip = dict(STRIPS)
    corners = jnp.concatenate(
        [got_mesh[strip[s]].astype(F32)[:B_CORNER] for s in CORNERS], 0
    ).astype(BF16)
    mesh_all = jnp.concatenate(
        [mesh_v[...]] + [got_mesh[strip[s]] for s in SIDES] + [corners], 0
    )
    mesh_table = jnp.concatenate([nn(mesh_all, w_mesh_v[...]), tail], 0) * 0.5
    table[:, grid_rows:] = jnp.transpose(mesh_table).astype(BF16)

    for start in range(0, edges, step):
        span = pl.ds(start, step)
        half = nn(table[...], onehot[:, span])
        hidden = (half + half * jnp.tanh(half)).astype(BF16)
        added = nt(onehot[grid_rows:, span], hidden)
        if start == 0:
            summed[...] = added
        else:
            summed[...] += added

    for s in SIDES:
        first = side_base + B_SIDE * SIDES.index(s)
        put_sum[strip[s]] = summed[first : first + B_SIDE, :].astype(BF16)
    for s in CORNERS:
        first = corner_base + B_CORNER * CORNERS.index(s)
        part = summed[first : first + B_CORNER, :]
        rest = jnp.zeros((B_SIDE - B_CORNER, features), F32)
        put_sum[strip[s]] = jnp.concatenate([part, rest], 0).astype(BF16)
    for dlat in (-1, 1, 0):

        def send(dlat=dlat):
            for s, k in in_band(dlat):
                sum_copy(s, k).start()

        guarded(dlat, send)

    loaded(w_message_v)
    loaded(w_output_v)
    loaded(gain_v)
    loaded(nbias_v)
    for dlat in (-1, 0, 1):

        def arrive(dlat=dlat):
            for s, k in in_band(dlat):
                sum_copy(s, k).wait_recv()

        def nothing(dlat=dlat):
            for s, k in in_band(dlat):
                got_sum[k] = jnp.zeros(got_sum.shape[1:], BF16)

        guarded(-dlat, arrive, nothing)

    border = 8 * B_SIDE
    arrived = got_sum[...].astype(F32).reshape(border, features)
    total = summed[:rows, :]
    total = jnp.concatenate([total[:border] + arrived, total[border:]], 0)
    high, low = halves(total)
    gathered = nn(high, w_message_v[...]) + nn(low, w_message_v[...])
    node = node_own + nn(gathered.astype(BF16), w_node_v[features:, :])
    node_hidden = (node * jax.nn.sigmoid(node)).astype(BF16)
    update = nn(node_hidden, w_output_v[...])
    row_mean = jnp.mean(update, axis=-1, keepdims=True)
    centered = update - row_mean
    row_var = jnp.mean(centered * centered, axis=-1, keepdims=True)
    normed = centered * lax.rsqrt(row_var + 1e-05) * gain_v[...] + nbias_v[...]
    out_ref[0, 0] = (mesh_v[...].astype(F32) + normed).astype(BF16)

    for dlat in (-1, 0, 1):

        def sent(dlat=dlat):
            for s, k in in_band(dlat):
                mesh_copy(s, k).wait_send()

        def sent_sum(dlat=dlat):
            for s, k in in_band(dlat):
                sum_copy(s, k).wait_send()

        guarded(-dlat, sent)
        guarded(dlat, sent_sum)


def local(n_lon, n_lat, *args):
    args = [a.reshape(1, -1) if a.ndim == 1 else a for a in args]
    grid_latent, mesh_latent, geometry, senders = args[:4]
    rows, features = mesh_latent.shape[2:]
    grid_rows = grid_latent.shape[2]
    edges = senders.shape[2]
    slots = rows + 4 * B_SIDE + 4 * B_CORNER
    wide = grid_rows + slots + TAIL
    loads = []
    for number, a in enumerate(args):
        shape = a.shape[2:] if number < 3 else a.shape[1:] if number < 5 else a.shape
        loads.append(pltpu.VMEM(shape, a.dtype))
    return pl.pallas_call(
        functools.partial(kernel, n_lon, n_lat),
        out_shape=jax.ShapeDtypeStruct(mesh_latent.shape, BF16),
        in_specs=[pl.BlockSpec(memory_space=pl.ANY)] * len(args),
        out_specs=pl.BlockSpec(memory_space=pltpu.VMEM),
        scratch_shapes=loads
        + [
            pltpu.VMEM((features, wide), BF16),
            pltpu.VMEM((wide, edges), BF16),
            pltpu.VMEM((slots + TAIL, features), F32),
            pltpu.VMEM((8, B_SIDE, features), BF16),
            pltpu.VMEM((8, B_SIDE, features), BF16),
            pltpu.VMEM((8, B_SIDE, features), BF16),
            pltpu.SemaphoreType.DMA((len(args),)),
            pltpu.SemaphoreType.DMA((8,)),
            pltpu.SemaphoreType.DMA((8,)),
            pltpu.SemaphoreType.DMA((8,)),
            pltpu.SemaphoreType.DMA((8,)),
        ],
        compiler_params=pltpu.CompilerParams(
            collective_id=0, has_side_effects=True, vmem_limit_bytes=56 * 1024 * 1024
        ),
    )(*args)


def solution(mesh):
    return jax.shard_map(
        functools.partial(local, mesh.shape["lon"], mesh.shape["lat"]),
        mesh=mesh,
        in_specs=(
            P("lat", "lon", None, None),
            P("lat", "lon", None, None),
            P("lat", "lon", None, None),
            P("lat", "lon", None),
            P("lat", "lon", None),
            P(),
            P(),
            P(),
            P(),
            P(),
            P(),
            P(),
            P(),
            P(),
        ),
        out_specs=P("lat", "lon", None, None),
        check_vma=False,
    )
```

time: 78.9 us -> 20.6 us (0.26)
  matrix products: 25.8 us -> 0 us
  local copies, waits for them, and re-layouts: 26.4 us -> 1.59 us
  Pallas kernels: 0 us -> 18.9 us
  starting transfers between devices: 14.5 us -> 0 us
  waiting for transfers between devices: 8.01 us -> 0 us
  other arithmetic: 3.05 us -> 0 us
    dot_general x11 -> x0, matrix products: 25.8 us -> none  [the longest x4 13.8 us: add_block(): jnp.dot(block_geometry.T, w_edge, precision=lax.Precision.HIGHEST)]
    gather x8 -> x0, local copies, waits for them, and re-layouts: 23.8 us -> none  [the longest x4 17.3 us: add_block(): grid_term = jnp.take(grid_proj, block_sources, axis=0)]
    pallas_call x0 -> x1, Pallas kernels: none -> 18.9 us  [local(): pl.pallas_call(functools.partial(kernel, n_lon, n_lat), out_shape=jax.Sha...]
    ppermute x8 -> x0, starting transfers between devices: 14.5 us -> none  [the longest x4 9.99 us: extended(): lax.ppermute(lax.slice_in_dim(block, 0, width, axis=dim), axis, backward)]
    ppermute x8 -> x0, waiting for transfers between devices: 8.01 us -> none  [the longest x4 6.36 us: extended(): lax.ppermute(lax.slice_in_dim(block, block.shape[dim] - width, None, axis...]
    another operation x4 -> x0, local copies, waits for them, and re-layouts: 1.03 us -> none  [the longest x2 1.01 us: mirrored_cells(): rows_out.append(jnp.stack(cells))]
    broadcast_in_dim x1 -> x0, other arithmetic: 0.83 us -> none  [local(): return mesh_out[None, None]]
    unnamed x39 -> x1, local copies, waits for them, and re-layouts: 1.53 us -> 1.59 us
  transfers between devices with their start and end apart: 8 -> 0, of which waited for: 5 -> 0; matrix products, arithmetic and copies ran while one was open for 8% -> 0% of each run, Pallas kernels for 0% -> 0%
where the time goes in v1:
time: 20.6 us; the launch traced here: 20.5 us
  Pallas kernels  18.9 us (92%)
  local copies, waits for them, and re-layouts  1.59 us (8%)
    pallas_call x1, Pallas kernels, local(): pl.pallas_call(functools.partial(kernel, n_lon, n_lat), out_shape=jax.Sha...  18.9 us
    unnamed x1, local copies, waits for them, and re-layouts  1.59 us

profile of v1, /device:TPU:0, one launch (start us, length us, event | category | flops | bytes accessed | tf_op | source)
XLA Modules:
  0.0 20.5 jit_solution(15439410581892601509)
XLA Ops:
  0.0 18.9 %shard_map.136 = bf16[1,1,160,512]{3,2,1,0:T(8,128)(2,1)} custom-call(bf16[1,1,1024,512]{3,2,1,0:T(8,128)(2,1)} %grid_h.1, bf16[1,1,160,512]{3,2,1,0:T(8,128)(2,1)} %mesh_h.1, f32[1,1,4,2048]{3,2,1,0:T(4,128)} %geo_h.1, s32[1,1,2048]{2,1,0:T(1,128)} %snd_h.1, s32[1,1,2048]{2,1,0:T(1,128)} %rcv_h.1, bf16[512,512]{1,0:T(8,128)(2,1)} %w_grid_h.1, ...), custom_call_target="tpu_custom_call" | custom-call | tf_op jit(solution)/shard_map/pallas_call | solution.py:333
  18.9 1.6 %copy.16 = bf16[1,1,160,512]{3,2,1,0:T(8,128)(2,1)} copy(bf16[1,1,160,512]{3,2,1,0:T(8,128)(2,1)} %shard_map.136) | data formatting | bytes 327680

commit v2 on v1

--- a/solution.py
+++ b/solution.py
@@ -10,6 +10,7 @@
 B_SIDE = 16
 B_CORNER = 4
 TAIL = 16
+OFFER_AT = 0
 MESH = pl.DeviceIdType.MESH
 
 BF16 = jnp.bfloat16
@@ -67,6 +68,7 @@
     nbias_v,
     table,
     onehot,
+    from_grid,
     summed,
     got_mesh,
     put_sum,
@@ -87,14 +89,14 @@
     slots = corner_base + 4 * B_CORNER
 
     sources = [
+        (snd_h.at[0], snd_v),
+        (w_grid_h, w_grid_v),
+        (grid_h.at[0, 0], grid_v),
         (mesh_h.at[0, 0], mesh_v),
-        (snd_h.at[0], snd_v),
         (rcv_h.at[0], rcv_v),
         (geo_h.at[0, 0], geo_v),
         (w_edge_h, w_edge_v),
         (bias_h, bias_v),
-        (w_grid_h, w_grid_v),
-        (grid_h.at[0, 0], grid_v),
         (w_mesh_h, w_mesh_v),
         (w_node_h, w_node_v),
         (w_message_h, w_message_v),
@@ -142,13 +144,14 @@
                     )
 
         guarded(dlat, greet)
-    arrivals = 2 + 3 * (lat > 0).astype(jnp.int32) + 3 * (lat < n_lat - 1).astype(jnp.int32)
-    pl.semaphore_wait(barrier, arrivals)
+
+    def size_of(slot):
+        return B_SIDE if slot in SIDES else B_CORNER
 
     def mesh_copy(slot, k):
         return pltpu.make_async_remote_copy(
-            src_ref=mesh_v.at[pl.ds(k * B_SIDE, B_SIDE)],
-            dst_ref=got_mesh.at[k],
+            src_ref=mesh_v.at[pl.ds(k * B_SIDE, size_of(slot))],
+            dst_ref=got_mesh.at[k, pl.ds(0, size_of(slot))],
             send_sem=send_a.at[k],
             recv_sem=recv_a.at[k],
             device_id=there(-(slot // 3 - 1), -(slot % 3 - 1)),
@@ -157,8 +160,8 @@
 
     def sum_copy(slot, k):
         return pltpu.make_async_remote_copy(
-            src_ref=put_sum.at[k],
-            dst_ref=got_sum.at[k],
+            src_ref=put_sum.at[k, pl.ds(0, size_of(slot))],
+            dst_ref=got_sum.at[k, pl.ds(0, size_of(slot))],
             send_sem=send_b.at[k],
             recv_sem=recv_b.at[k],
             device_id=there(slot // 3 - 1, slot % 3 - 1),
@@ -168,16 +171,37 @@
     def in_band(dlat):
         return [(s, k) for s, k in STRIPS if s // 3 - 1 == dlat]
 
+    def offer_strips():
+        arrivals = 2 + 3 * (lat > 0).astype(jnp.int32) + 3 * (lat < n_lat - 1).astype(jnp.int32)
+        pl.semaphore_wait(barrier, arrivals)
+        for dlat in (-1, 1, 0):
+
+            def send(dlat=dlat):
+                for s, k in in_band(dlat):
+                    mesh_copy(s, k).start()
+
+            guarded(-dlat, send)
+
+    step = min(512, edges)
+    starts = list(range(0, edges, step))
+    loaded(snd_v)
+    for start in starts:
+        span = pl.ds(start, step)
+        ids = lax.broadcasted_iota(jnp.int32, (grid_rows, step), 0)
+        onehot[:grid_rows, span] = jnp.where(ids == snd_v[:, span], 1.0, 0.0).astype(BF16)
+    loaded(w_grid_v)
+    w_grid_t = jnp.transpose(w_grid_v[...])
+    loaded(grid_v)
+    table[:, :grid_rows] = (0.5 * nt(w_grid_t, grid_v[...])).astype(BF16)
     loaded(mesh_v)
-    for dlat in (-1, 1, 0):
-
-        def send(dlat=dlat):
-            for s, k in in_band(dlat):
-                mesh_copy(s, k).start()
-
-        guarded(-dlat, send)
-
-    loaded(snd_v)
+    for number, start in enumerate(starts):
+        if number == OFFER_AT:
+            offer_strips()
+        span = pl.ds(start, step)
+        from_grid[:, span] = nn(table[:, :grid_rows], onehot[:grid_rows, span])
+    if OFFER_AT >= len(starts):
+        offer_strips()
+
     loaded(rcv_v)
     loaded(geo_v)
     picks = rcv_v[...]
@@ -195,11 +219,8 @@
         else:
             spot = spot + jnp.where(picks >= s * rows, base - shift, 0)
         shift = base
-    step = min(512, edges)
-    for start in range(0, edges, step):
+    for start in starts:
         span = pl.ds(start, step)
-        ids = lax.broadcasted_iota(jnp.int32, (grid_rows, step), 0)
-        onehot[:grid_rows, span] = jnp.where(ids == snd_v[:, span], 1.0, 0.0).astype(BF16)
         ids = lax.broadcasted_iota(jnp.int32, (slots, step), 0)
         onehot[grid_rows : grid_rows + slots, span] = jnp.where(
             ids == spot[:, start : start + step], 1.0, 0.0
@@ -208,11 +229,6 @@
     ones = jnp.ones((2, edges), F32)
     zeros = jnp.zeros((2, edges), F32)
     onehot[grid_rows + slots :, :] = jnp.concatenate([high, high, low, ones, zeros], 0).astype(BF16)
-
-    loaded(w_grid_v)
-    loaded(grid_v)
-    w_grid_t = jnp.transpose(w_grid_v[...])
-    table[:, :grid_rows] = (0.5 * nt(w_grid_t, grid_v[...])).astype(BF16)
 
     loaded(w_edge_v)
     loaded(bias_v)
@@ -223,6 +239,10 @@
     )
     loaded(w_mesh_v)
     loaded(w_node_v)
+    loaded(w_message_v)
+    loaded(w_output_v)
+    loaded(gain_v)
+    loaded(nbias_v)
     node_own = nn(mesh_v[...], w_node_v[:features, :])
 
     for dlat in (-1, 0, 1):
@@ -249,7 +269,7 @@
 
     for start in range(0, edges, step):
         span = pl.ds(start, step)
-        half = nn(table[...], onehot[:, span])
+        half = from_grid[:, span] + nn(table[:, grid_rows:], onehot[grid_rows:, span])
         hidden = (half + half * jnp.tanh(half)).astype(BF16)
         added = nt(onehot[grid_rows:, span], hidden)
         if start == 0:
@@ -273,10 +293,8 @@
 
         guarded(dlat, send)
 
-    loaded(w_message_v)
-    loaded(w_output_v)
-    loaded(gain_v)
-    loaded(nbias_v)
+    high, low = halves(summed[:rows, :])
+    own_message = nn(high, w_message_v[...]) + nn(low, w_message_v[...])
     for dlat in (-1, 0, 1):
 
         def arrive(dlat=dlat):
@@ -290,11 +308,17 @@
         guarded(-dlat, arrive, nothing)
 
     border = 8 * B_SIDE
-    arrived = got_sum[...].astype(F32).reshape(border, features)
-    total = summed[:rows, :]
-    total = jnp.concatenate([total[:border] + arrived, total[border:]], 0)
-    high, low = halves(total)
-    gathered = nn(high, w_message_v[...]) + nn(low, w_message_v[...])
+    pieces = []
+    for s, k in STRIPS:
+        piece = got_sum[k]
+        if s in CORNERS:
+            rest = jnp.zeros((B_SIDE - B_CORNER, features), F32)
+            piece = jnp.concatenate([piece.astype(F32)[:B_CORNER], rest], 0).astype(BF16)
+        pieces.append(piece)
+    border_message = nn(jnp.concatenate(pieces, 0), w_message_v[...])
+    gathered = jnp.concatenate(
+        [own_message[:border] + border_message, own_message[border:]], 0
+    )
     node = node_own + nn(gathered.astype(BF16), w_node_v[features:, :])
     node_hidden = (node * jax.nn.sigmoid(node)).astype(BF16)
     update = nn(node_hidden, w_output_v[...])
@@ -332,13 +356,14 @@
         loads.append(pltpu.VMEM(shape, a.dtype))
     return pl.pallas_call(
         functools.partial(kernel, n_lon, n_lat),
-        out_shape=jax.ShapeDtypeStruct(mesh_latent.shape, BF16),
+        out_shape=pltpu.VMEM(mesh_latent.shape, BF16),
         in_specs=[pl.BlockSpec(memory_space=pl.ANY)] * len(args),
         out_specs=pl.BlockSpec(memory_space=pltpu.VMEM),
         scratch_shapes=loads
         + [
             pltpu.VMEM((features, wide), BF16),
             pltpu.VMEM((wide, edges), BF16),
+            pltpu.VMEM((features, edges), F32),
             pltpu.VMEM((slots + TAIL, features), F32),
             pltpu.VMEM((8, B_SIDE, features), BF16),
             pltpu.VMEM((8, B_SIDE, features), BF16),

time: 20.6 us -> 16.2 us (0.79)
  Pallas kernels: 18.9 us -> 15.4 us
  local copies, waits for them, and re-layouts: 1.59 us -> 0.67 us
    pallas_call x1, Pallas kernels: 18.9 us -> 15.4 us  [local(): pl.pallas_call(functools.partial(kernel, n_lon, n_lat), out_shape=pltpu.V...]
    unnamed x1, local copies, waits for them, and re-layouts: 1.59 us -> 0.67 us
where the time goes in v2:
time: 16.2 us; the launch traced here: 16.1 us
  Pallas kernels  15.4 us (95%)
  local copies, waits for them, and re-layouts  0.67 us (4%)
    pallas_call x1, Pallas kernels, local(): pl.pallas_call(functools.partial(kernel, n_lon, n_lat), out_shape=pltpu.V...  15.4 us
    unnamed x1, local copies, waits for them, and re-layouts  0.67 us

profile of v2, /device:TPU:0, one launch (start us, length us, event | category | flops | bytes accessed | tf_op | source)
XLA Modules:
  0.0 16.1 jit_solution(1291902422683583846)
XLA Ops:
  0.0 15.4 %shard_map.136 = bf16[1,1,160,512]{3,2,1,0:T(8,128)(2,1)S(1)} custom-call(bf16[1,1,1024,512]{3,2,1,0:T(8,128)(2,1)} %grid_h.1, bf16[1,1,160,512]{3,2,1,0:T(8,128)(2,1)} %mesh_h.1, f32[1,1,4,2048]{3,2,1,0:T(4,128)} %geo_h.1, s32[1,1,2048]{2,1,0:T(1,128)} %snd_h.1, s32[1,1,2048]{2,1,0:T(1,128)} %rcv_h.1, bf16[512,512]{1,0:T(8,128)(2,1)} %w_grid_h.1, ...), custom_call_target="tpu_custom_call" | custom-call | tf_op jit(solution)/shard_map/pallas_call | solution.py:357
  15.4 0.7 %copy.16 = bf16[1,1,160,512]{3,2,1,0:T(8,128)(2,1)} copy(bf16[1,1,160,512]{3,2,1,0:T(8,128)(2,1)S(1)} %shard_map.136) | data formatting | bytes 327680
